TPU v7x, 32 devices: a whole 2x2x4 slice. The times are simulated.
32 devices in a mesh: section: 2 (over y), row: 4 (over x, core), col: 4 (over z).
Axes of the slice: x: 2, y: 2, z: 4, core: 2. Of those that a mesh axis runs over, the one named last changes fastest.
Arguments:
- inputs: float32 [3, 128, 16384], P(None, None, ('row', 'col')), may hold values from -512 to 512
- weights: float32 [2, 4, 4, 1024, 16384], P('section', None, 'col', None, 'row'), may hold values from -1 to 1
- norm_gain: float32 [2, 16384], P('section', ('row', 'col')), may hold values from 0.5 to 1.5
Outputs:
- section_outputs: float32 [2, 3, 128, 16384], P('section', None, None, ('row', 'col'))
All inputs are finite; a program needn't handle non-finite values.
Results may differ from a plain program's by a relative error of at most 0.00036.
Values sent between devices are 32-bit elements; how exact they have to be, the bound alone decides.
A program may use at most 192 MiB of HBM per device.

v0:
```python
import jax
import jax.numpy as jnp
from jax import lax
from jax.sharding import PartitionSpec as P


def from_behind(value, axis, steps):
    count = lax.axis_size(axis)
    initial, last = (max(0, -steps), min(count, count - steps))
    return lax.ppermute(value, axis, [(source, source + steps) for source in range(initial, last)])


def split_two(values):
    first = lax.optimization_barrier(values.astype(jnp.bfloat16))
    second = lax.optimization_barrier((values - first.astype(jnp.float32)).astype(jnp.bfloat16))
    return (first, second)


def shards(inputs, weights, norm_gain):
    section_id = lax.axis_index("section")
    row_count = lax.axis_size("row")
    pieces = weights.shape[3]
    out_cols = weights.shape[4]
    flat = weights.reshape(row_count * pieces, out_cols)
    wfirst, wsecond = split_two(flat)
    micro = inputs.shape[0]
    rows = inputs.shape[1]
    gain = norm_gain[0]
    total_features = out_cols * row_count
    received = jnp.zeros((rows, pieces), jnp.float32)
    results = jnp.zeros((micro, rows, pieces), jnp.float32)
    for step in range(micro + 1):
        fresh = inputs[min(step, micro - 1)]
        earlier = inputs[max(step - 1, 0)]
        current = jnp.where(section_id == 0, fresh, earlier + received)
        first, second = split_two(lax.all_gather(current, "row", axis=1, tiled=True))
        double = jnp.concatenate([first, second], axis=0)
        prod_one = jnp.dot(double, wfirst, preferred_element_type=jnp.float32)
        prod_two = jnp.dot(first, wsecond, preferred_element_type=jnp.float32)
        partial_value = prod_one[:rows] + prod_one[rows:] + prod_two
        summed = lax.psum_scatter(partial_value, "col", scatter_dimension=1, tiled=True)
        active = jax.nn.gelu(summed, approximate=True)
        squares = lax.psum(jnp.sum(active * active, axis=1), ("row", "col"))
        scale = lax.rsqrt(squares / total_features + 1e-06)
        normed = active * scale[:, None] * gain[None, :]
        position = step - section_id
        valid = jnp.logical_and(position >= 0, position < micro)
        place = jnp.clip(position, 0, micro - 1)
        former = lax.dynamic_index_in_dim(results, place, 0, keepdims=False)
        results = lax.dynamic_update_index_in_dim(
            results, jnp.where(valid, normed, former), place, 0
        )
        if step < micro:
            received = from_behind(normed, "section", 1)
    return results[None]


def solution(mesh):
    placed = (
        P(None, None, ("row", "col")),
        P("section", None, "col", None, "row"),
        P("section", ("row", "col")),
    )
    return jax.shard_map(
        shards,
        mesh=mesh,
        in_specs=placed,
        out_specs=P("section", None, None, ("row", "col")),
        check_vma=False,
    )
```

profile of v0, /device:TPU:5, one launch (start us, length us, event | category | flops | bytes accessed | tf_op | source)
XLA Modules:
  0.0 654.6 jit_solution(15960127548872160041)
XLA Ops:
  8.5 32.9 %bitcast_convert_fusion = bf16[4096,4096]{1,0:T(8,128)(2,1)} fusion(f32[1,4,1,1024,4096]{4,3,2,1,0:T(8,128)} %param.4), kind=kLoop, calls=%fused_computation.1 | loop fusion | flops 16777216 | bytes 100663296 | tf_op jit(solution)/shard_map/convert_element_type | solution.py:14
  41.4 42.3 %fusion = bf16[4096,4096]{1,0:T(8,128)(2,1)} fusion(f32[1,4,1,1024,4096]{4,3,2,1,0:T(8,128)} %param.4, bf16[4096,4096]{1,0:T(8,128)(2,1)} %bitcast_convert_fusion), kind=kLoop, calls=%fused_computation.2 | loop fusion | flops 50331648 | bytes 134217728 | tf_op jit(solution)/shard_map/convert_element_type | solution.py:15
  86.2 15.1 %fusion.2 = f32[256,4096]{1,0:T(8,128)S(1)} fusion(bf16[4096,4096]{1,0:T(8,128)(2,1)} %bitcast_convert_fusion, bf16[128,4096]{1,0:T(8,128)(2,1)S(1)} %fusion.18, bf16[128,4096]{1,0:T(8,128)(2,1)S(1)} %bitcast_convert_fusion.1), kind=kOutput, calls=%fused_computation.12 | convolution fusion | flops 8594128896 | bytes 39845888 | tf_op jit(solution)/shard_map/dot_general | solution.py:38
  101.3 16.6 %fusion.1 = f32[128,4096]{1,0:T(8,128)} fusion(bf16[128,4096]{1,0:T(8,128)(2,1)S(1)} %bitcast_convert_fusion.1, bf16[4096,4096]{1,0:T(8,128)(2,1)} %fusion, f32[256,4096]{1,0:T(8,128)S(1)} %fusion.2), kind=kOutput, calls=%fused_computation.4 | convolution fusion | flops 4296015872 | bytes 40894464 | tf_op jit(solution)/shard_map/dot_general | solution.py:39
  118.1 44.4 %reduce-scatter.5.cloned.1.call-done = f32[128,1024]{1,0:T(8,128)} async-done(((f32[128,4096]{1,0:T(8,128)}), f32[128,1024]{1,0:T(8,128)}) %reduce-scatter.5.cloned.1.call-update) | async-done | bytes 524304 | tf_op jit(solution)/shard_map/reduce_scatter | solution.py:41
  163.8 29.0 %psum.28 = f32[128]{0:T(128)S(1)} all-reduce(f32[128]{0:T(128)S(1)} %multiply_reduce_fusion.3), channel_id=1, replica_groups=mesh['section'=2,'row'=4,'col'=4] {'row','col'}, use_global_device_ids=true, to_apply=%region_2.3 | all-reduce | flops 128 | bytes 1024 | tf_op jit(solution)/shard_map/psum | solution.py:43
  196.4 10.9 %collective-permute-done = f32[128,1024]{1,0:T(8,128)} collective-permute-done((f32[128,1024]{1,0:T(8,128)}, f32[128,1024]{1,0:T(8,128)}, u32[]{:S(2)}, u32[]{:S(2)}) %collective-permute-start) | collective-permute-done | bytes 524320 | tf_op jit(solution)/shard_map/ppermute | solution.py:10
  209.4 26.2 %all-gather.6.cloned.1.call-done = f32[128,4096]{1,0:T(8,128)} async-done(((f32[128,1024]{1,0:T(8,128)}), f32[128,4096]{1,0:T(8,128)}) %all-gather.6.cloned.1.call-update) | async-done | bytes 2097168 | tf_op jit(solution)/shard_map/all_gather | solution.py:36
  238.0 16.1 %fusion.6 = f32[256,4096]{1,0:T(8,128)} fusion(bf16[4096,4096]{1,0:T(8,128)(2,1)} %bitcast_convert_fusion, bf16[128,4096]{1,0:T(8,128)(2,1)S(1)} %subtract_convert_fusion.2, bf16[128,4096]{1,0:T(8,128)(2,1)S(1)} %convert_element_type.51), kind=kOutput, calls=%fused_computation.16 | convolution fusion | flops 8594128896 | bytes 39845888 | tf_op jit(solution)/shard_map/dot_general | solution.py:38
  254.1 17.8 %convolution_add_fusion.2 = f32[128,4096]{1,0:T(8,128)} fusion(bf16[128,4096]{1,0:T(8,128)(2,1)S(1)} %convert_element_type.51, bf16[4096,4096]{1,0:T(8,128)(2,1)} %fusion, f32[256,4096]{1,0:T(8,128)} %fusion.6), kind=kOutput, calls=%fused_computation.7 | convolution fusion | flops 4296015872 | bytes 40894464 | tf_op jit(solution)/shard_map/dot_general | solution.py:39
  272.8 42.1 %reduce-scatter.7.cloned.1.call-done = f32[128,1024]{1,0:T(8,128)} async-done(((f32[128,4096]{1,0:T(8,128)}), f32[128,1024]{1,0:T(8,128)}) %reduce-scatter.7.cloned.1.call-update) | async-done | bytes 524304 | tf_op jit(solution)/shard_map/reduce_scatter | solution.py:41
  316.2 29.0 %psum.29 = f32[128]{0:T(128)S(1)} all-reduce(f32[128]{0:T(128)S(1)} %multiply_reduce_fusion.2), channel_id=1, replica_groups=mesh['section'=2,'row'=4,'col'=4] {'row','col'}, use_global_device_ids=true, to_apply=%region_5.6 | all-reduce | flops 128 | bytes 1024 | tf_op jit(solution)/shard_map/psum | solution.py:43
  347.9 10.6 %collective-permute-done.1 = f32[128,1024]{1,0:T(8,128)S(1)} collective-permute-done((f32[128,1024]{1,0:T(8,128)S(1)}, f32[128,1024]{1,0:T(8,128)S(1)}, u32[]{:S(2)}, u32[]{:S(2)}) %collective-permute-start.1) | collective-permute-done | bytes 524320 | tf_op jit(solution)/shard_map/ppermute | solution.py:10
  359.7 26.1 %all-gather.8.cloned.1.call-done = f32[128,4096]{1,0:T(8,128)} async-done(((f32[128,1024]{1,0:T(8,128)}), f32[128,4096]{1,0:T(8,128)}) %all-gather.8.cloned.1.call-update) | async-done | bytes 2097168 | tf_op jit(solution)/shard_map/all_gather | solution.py:36
  388.2 16.1 %fusion.10 = f32[256,4096]{1,0:T(8,128)} fusion(bf16[4096,4096]{1,0:T(8,128)(2,1)} %bitcast_convert_fusion, bf16[128,4096]{1,0:T(8,128)(2,1)S(1)} %subtract_convert_fusion.1, bf16[128,4096]{1,0:T(8,128)(2,1)S(1)} %convert_element_type.54), kind=kOutput, calls=%fused_computation.20 | convolution fusion | flops 8594128896 | bytes 39845888 | tf_op jit(solution)/shard_map/dot_general | solution.py:38
  404.3 17.8 %convolution_add_fusion.1 = f32[128,4096]{1,0:T(8,128)} fusion(bf16[128,4096]{1,0:T(8,128)(2,1)S(1)} %convert_element_type.54, bf16[4096,4096]{1,0:T(8,128)(2,1)} %fusion, f32[256,4096]{1,0:T(8,128)} %fusion.10), kind=kOutput, calls=%fused_computation.6 | convolution fusion | flops 4296015872 | bytes 40894464 | tf_op jit(solution)/shard_map/dot_general | solution.py:39
  423.0 42.1 %reduce-scatter.9.cloned.1.call-done = f32[128,1024]{1,0:T(8,128)} async-done(((f32[128,4096]{1,0:T(8,128)}), f32[128,1024]{1,0:T(8,128)}) %reduce-scatter.9.cloned.1.call-update) | async-done | bytes 524304 | tf_op jit(solution)/shard_map/reduce_scatter | solution.py:41
  466.4 29.0 %psum.30 = f32[128]{0:T(128)S(1)} all-reduce(f32[128]{0:T(128)S(1)} %multiply_reduce_fusion.1), channel_id=1, replica_groups=mesh['section'=2,'row'=4,'col'=4] {'row','col'}, use_global_device_ids=true, to_apply=%region_8.9 | all-reduce | flops 128 | bytes 1024 | tf_op jit(solution)/shard_map/psum | solution.py:43
  498.2 10.6 %collective-permute-done.2 = f32[128,1024]{1,0:T(8,128)S(1)} collective-permute-done((f32[128,1024]{1,0:T(8,128)S(1)}, f32[128,1024]{1,0:T(8,128)S(1)}, u32[]{:S(2)}, u32[]{:S(2)}) %collective-permute-start.2) | collective-permute-done | bytes 524320 | tf_op jit(solution)/shard_map/ppermute | solution.py:10
  509.9 26.0 %all-gather.10.cloned.1.call-done = f32[128,4096]{1,0:T(8,128)} async-done(((f32[128,1024]{1,0:T(8,128)}), f32[128,4096]{1,0:T(8,128)}) %all-gather.10.cloned.1.call-update) | async-done | bytes 2097168 | tf_op jit(solution)/shard_map/all_gather | solution.py:36
  538.4 16.1 %fusion.14 = f32[256,4096]{1,0:T(8,128)} fusion(bf16[4096,4096]{1,0:T(8,128)(2,1)} %bitcast_convert_fusion, bf16[128,4096]{1,0:T(8,128)(2,1)S(1)} %subtract_convert_fusion, bf16[128,4096]{1,0:T(8,128)(2,1)S(1)} %convert_element_type.57), kind=kOutput, calls=%fused_computation.24 | convolution fusion | flops 8594128896 | bytes 39845888 | tf_op jit(solution)/shard_map/dot_general | solution.py:38
  554.6 17.8 %convolution_add_fusion = f32[128,4096]{1,0:T(8,128)} fusion(bf16[128,4096]{1,0:T(8,128)(2,1)S(1)} %convert_element_type.57, bf16[4096,4096]{1,0:T(8,128)(2,1)} %fusion, f32[256,4096]{1,0:T(8,128)} %fusion.14), kind=kOutput, calls=%fused_computation.5 | convolution fusion | flops 4296015872 | bytes 40894464 | tf_op jit(solution)/shard_map/dot_general | solution.py:39
  573.5 41.8 %reduce-scatter.11.cloned.1.call-done = f32[128,1024]{1,0:T(8,128)} async-done(((f32[128,4096]{1,0:T(8,128)}), f32[128,1024]{1,0:T(8,128)}) %reduce-scatter.11.cloned.1.call-update) | async-done | bytes 524304 | tf_op jit(solution)/shard_map/reduce_scatter | solution.py:41
  616.7 29.0 %psum.31 = f32[128]{0:T(128)S(1)} all-reduce(f32[128]{0:T(128)S(1)} %multiply_reduce_fusion), channel_id=1, replica_groups=mesh['section'=2,'row'=4,'col'=4] {'row','col'}, use_global_device_ids=true, to_apply=%region_11.12 | all-reduce | flops 128 | bytes 1024 | tf_op jit(solution)/shard_map/psum | solution.py:43
  (60 shorter events, 35.5 us)
Async XLA Ops:
  6.5 77.2 %all-gather.12.cloned.1.call-start = ((), (), s32[]{:S(2)}) async-start(), calls=%async_computation.11 | async-start | bytes 2621440 | tf_op jit(solution)/shard_map/all_gather | solution.py:36
  8.4 154.0 %reduce-scatter.5.cloned.1.call-start = ((), (), s32[]{:S(2)}) async-start(), calls=%async_computation.4 | async-start | bytes 2621440 | tf_op jit(solution)/shard_map/reduce_scatter | solution.py:41
  83.8 2.2 copy-start
  118.0 75.0 %copy-start.5 = (f32[1,1024]{1,0:T(1,128)S(1)}, f32[1,1024]{1,0:T(1,128)}, u32[]{:S(2)}) copy-start(f32[1,1024]{1,0:T(1,128)} %param.5) | copy-start | bytes 12292
  118.0 89.2 %copy-start.4 = (f32[3,128,1024]{2,1,0:T(8,128)S(1)}, f32[3,128,1024]{2,1,0:T(8,128)}, u32[]{:S(2)}) copy-start(f32[3,128,1024]{2,1,0:T(8,128)} %param.3) | copy-start | bytes 4718596
  118.0 117.5 %all-gather.6.cloned.1.call-start = ((), (), s32[]{:S(2)}) async-start(), calls=%async_computation.5 | async-start | bytes 2621440 | tf_op jit(solution)/shard_map/all_gather | solution.py:36
  195.1 12.1 %collective-permute-start = (f32[128,1024]{1,0:T(8,128)}, f32[128,1024]{1,0:T(8,128)}, u32[]{:S(2)}, u32[]{:S(2)}) collective-permute-start(f32[128,1024]{1,0:T(8,128)} %get-tuple-element.10), channel_id=1, source_target_pairs={{0,16},{1,17},{2,18},{3,19},{4,20},{5,21},{6,22},{7,23},{8,24},{9,... | collective-permute-start | bytes 1572872 | tf_op jit(solution)/shard_map/ppermute | solution.py:10
  209.2 105.8 %reduce-scatter.7.cloned.1.call-start = ((), (), s32[]{:S(2)}) async-start(), calls=%async_computation.6 | async-start | bytes 2621440 | tf_op jit(solution)/shard_map/reduce_scatter | solution.py:41
  235.5 2.2 copy-start.1
  271.9 113.9 %all-gather.8.cloned.1.call-start = ((), (), s32[]{:S(2)}) async-start(), calls=%async_computation.7 | async-start | bytes 2621440 | tf_op jit(solution)/shard_map/all_gather | solution.py:36
  346.6 11.9 %collective-permute-start.1 = (f32[128,1024]{1,0:T(8,128)S(1)}, f32[128,1024]{1,0:T(8,128)S(1)}, u32[]{:S(2)}, u32[]{:S(2)}) collective-permute-start(f32[128,1024]{1,0:T(8,128)S(1)} %get-tuple-element.8), channel_id=1, source_target_pairs={{0,16},{1,17},{2,18},{3,19},{4,20},{5,21},{6,22},{7,23},{8,24},{9,... | collective-permute-start | bytes 1572872 | tf_op jit(solution)/shard_map/ppermute | solution.py:10
  359.4 105.7 %reduce-scatter.9.cloned.1.call-start = ((), (), s32[]{:S(2)}) async-start(), calls=%async_computation.8 | async-start | bytes 2621440 | tf_op jit(solution)/shard_map/reduce_scatter | solution.py:41
  385.8 2.2 copy-start.2
  422.1 113.8 %all-gather.10.cloned.1.call-start = ((), (), s32[]{:S(2)}) async-start(), calls=%async_computation.9 | async-start | bytes 2621440 | tf_op jit(solution)/shard_map/all_gather | solution.py:36
  496.9 11.9 %collective-permute-start.2 = (f32[128,1024]{1,0:T(8,128)S(1)}, f32[128,1024]{1,0:T(8,128)S(1)}, u32[]{:S(2)}, u32[]{:S(2)}) collective-permute-start(f32[128,1024]{1,0:T(8,128)S(1)} %get-tuple-element.6), channel_id=1, source_target_pairs={{0,16},{1,17},{2,18},{3,19},{4,20},{5,21},{6,22},{7,23},{8,24},{9,... | collective-permute-start | bytes 1572872 | tf_op jit(solution)/shard_map/ppermute | solution.py:10
  509.6 105.7 %reduce-scatter.11.cloned.1.call-start = ((), (), s32[]{:S(2)}) async-start(), calls=%async_computation.10 | async-start | bytes 2621440 | tf_op jit(solution)/shard_map/reduce_scatter | solution.py:41
  536.0 2.2 copy-start.3
Sparse Core Ops, SparseCore 0:
  8.9 24.1 all-gather.11
  118.1 44.3 reduce-scatter.4
  209.3 26.2 all-gather.5
  272.0 42.8 reduce-scatter.6
  359.5 26.1 all-gather.7
  422.2 42.8 reduce-scatter.8
  509.7 26.1 all-gather.9
  572.5 42.8 reduce-scatter.10
where the time goes:
time: 660 us; the launch traced here: 655 us
  waiting for transfers between devices  281 us (43%)
  matrix products  133 us (20%)
  blocking collectives  116 us (18%)
  other arithmetic  99.5 us (15%)
  between operations  13.7 us (2%)
    reduce_scatter x4, waiting for transfers between devices, shards(): lax.psum_scatter(partial_value, 'col', scatter_dimension=1, tiled=True)  170 us
    psum x4, blocking collectives, shards(): squares = lax.psum(jnp.sum(active * active, axis=1), ('row', 'col'))  116 us
    all_gather x4, waiting for transfers between devices, shards(): lax.all_gather(current, 'row', axis=1, tiled=True)  78.3 us
    dot_general x4, matrix products, shards(): prod_two = jnp.dot(first, wsecond, preferred_element_type=jnp.float32)  70 us
    dot_general x4, matrix products, shards(): prod_one = jnp.dot(double, wfirst, preferred_element_type=jnp.float32)  63.4 us
    convert_element_type x5, other arithmetic, split_two(): (values - first.astype(jnp.float32)).astype(jnp.bfloat16)  43.2 us
    convert_element_type x5, other arithmetic, split_two(): first = lax.optimization_barrier(values.astype(jnp.bfloat16))  40.4 us
    ppermute x3, waiting for transfers between devices, from_behind(): lax.ppermute(value, axis, [(source, source + steps) for source in range(i...  32 us
  transfers between devices with their start and end apart: 11, of which 10 were waited for; matrix products, arithmetic and copies ran while one was open for 12% of the time, Pallas kernels for 0%

commit v1 on v0

v1 whole, which is shorter than its diff:
```python
import functools

import jax
import jax.numpy as jnp
from jax import lax
from jax.experimental import pallas as pl
from jax.experimental.pallas import tpu as pltpu
from jax.sharding import PartitionSpec as P

MESH = pl.DeviceIdType.MESH
GROUP = 16
SLOTS = 4


def slices(values):
    first = values.astype(jnp.bfloat16)
    second = (values - first.astype(jnp.float32)).astype(jnp.bfloat16)
    return first, second


def kernel(
    sections, row_count, col_count,
    x_ref, w_ref, gain_ref, out_ref,
    gathered, lhs, part, landed, active, squares, handed, handing, tiles,
    col_out, col_in, row_out, row_in,
    tile_sem, ag_send, ag_recv, rs_send, rs_recv,
    col_send, col_recv, row_send, row_recv, next_send, next_recv,
):
    micro, rows, pieces = x_ref.shape
    width = tiles.shape[2]
    per_chunk = pieces // width
    per_micro = per_chunk * col_count
    total_features = pieces * row_count * col_count
    section = lax.axis_index("section")
    row = lax.axis_index("row")
    col = lax.axis_index("col")
    cores = 2 if row_count % 2 == 0 else 1
    chips = row_count // cores
    core = lax.rem(row, cores)
    chip = row // cores

    def around(position, step, count):
        return lax.rem(position + step, count)

    def chip_row(step, which):
        return around(chip, step, chips) * cores + which

    def remote(src, dst, send, recv, device):
        return pltpu.make_async_remote_copy(
            src_ref=src, dst_ref=dst, send_sem=send, recv_sem=recv,
            device_id=device, device_id_type=MESH,
        )

    def fetch(step):
        within = lax.rem(step, per_micro)
        chunk = around(col, 1 + within // per_chunk, col_count)
        start = chunk * pieces + lax.rem(within, per_chunk) * width
        slot = lax.rem(step, SLOTS)
        return pltpu.make_async_copy(
            w_ref.at[:, pl.ds(pl.multiple_of(start, width), width)],
            tiles.at[slot], tile_sem.at[slot],
        )

    for step in range(SLOTS - 1):
        fetch(step).start()

    barrier = pltpu.get_barrier_semaphore()
    for step in range(1, row_count):
        pl.semaphore_signal(barrier, inc=1, device_id={"row": around(row, step, row_count)}, device_id_type=MESH)
    for step in range(1, col_count):
        pl.semaphore_signal(barrier, inc=1, device_id={"col": around(col, step, col_count)}, device_id_type=MESH)

    @pl.when(section > 0)
    def _():
        pl.semaphore_signal(barrier, inc=1, device_id={"section": section - 1}, device_id_type=MESH)

    @pl.when(section < sections - 1)
    def _():
        pl.semaphore_signal(barrier, inc=1, device_id={"section": section + 1}, device_id_type=MESH)

    before = (section + sections - 1) // sections
    after = (2 * (sections - 1) - section) // sections
    pl.semaphore_wait(barrier, row_count + col_count - 2 + before + after)

    def gather_send(m, source, target):
        return remote(source, gathered.at[m, row], ag_send.at[m, target], ag_recv.at[m, row], {"row": target})

    def gather_start(m, source):
        gathered[m, row] = source[...]
        for step in range(1, chips):
            gather_send(m, source, chip_row(step, core)).start()
        if cores == 2:
            gather_send(m, source, chip * cores + 1 - core).start()

    def gather_forward(m, step):
        held = chip_row(step, core)
        slot = chip_row(step, 1 - core)
        return remote(
            gathered.at[m, held], gathered.at[m, held], ag_send.at[m, slot],
            ag_recv.at[m, held], {"row": chip * cores + 1 - core},
        )

    def gather_landed(m, source):
        target = around(row, 1, row_count)
        remote(gathered.at[m, source], gathered.at[m, source], ag_send.at[m, source],
               ag_recv.at[m, source], {"row": target}).wait_recv()

    def hand(m):
        return remote(handing.at[m], handed.at[m], next_send.at[m], next_recv.at[m], {"section": section + 1})

    def chunk_send(m, chunk):
        return remote(part.at[m, chunk], landed.at[m, col], rs_send.at[m, chunk], rs_recv.at[m, col], {"col": chunk})

    @pl.when(section == 0)
    def _():
        def begin(m, carry):
            gather_start(m, x_ref.at[m])
            return carry
        lax.fori_loop(0, micro, begin, 0)

    def multiply(m):
        @pl.when(section > 0)
        def _():
            remote(handing.at[m], handed.at[m], next_send.at[m], next_recv.at[m], {"section": section - 1}).wait_recv()
            gather_start(m, handed.at[m])

        for step in range(1, chips):
            gather_landed(m, chip_row(step, core))
            if cores == 2:
                gather_forward(m, step).start()
        if cores == 2:
            for step in range(chips):
                gather_landed(m, chip_row(step, 1 - core))

        def prepare(r, carry):
            first, second = slices(gathered[m, r])
            lhs[r, :rows] = first
            lhs[r, rows:] = second
            return carry
        lax.fori_loop(0, row_count, prepare, 0)

        def chunk_body(i, carry):
            chunk = around(col, 1 + i, col_count)

            def tile_body(j, carry):
                step = m * per_micro + i * per_chunk + j
                slot = lax.rem(step, SLOTS)

                @pl.when(step + SLOTS - 1 < micro * per_micro)
                def _():
                    fetch(step + SLOTS - 1).start()

                fetch(step).wait()
                both = jnp.zeros((2 * rows, width), jnp.float32)
                low = jnp.zeros((rows, width), jnp.float32)
                for r in range(row_count):
                    first, second = slices(tiles[slot, r * pieces:(r + 1) * pieces, :])
                    both += jnp.dot(lhs[r], first, preferred_element_type=jnp.float32)
                    low += jnp.dot(lhs[r, :rows], second, preferred_element_type=jnp.float32)
                part[m, chunk, :, pl.ds(pl.multiple_of(j * width, width), width)] = both[:rows] + (both[rows:] + low)
                return carry
            lax.fori_loop(0, per_chunk, tile_body, 0)

            @pl.when(i < col_count - 1)
            def _():
                chunk_send(m, chunk).start()
            return carry
        lax.fori_loop(0, col_count, chunk_body, 0)

    def finish(m):
        for step in range(1, col_count):
            source = around(col, step, col_count)
            remote(part.at[m, source], landed.at[m, source], rs_send.at[m, source],
                   rs_recv.at[m, source], {"col": source}).wait_recv()

        def activate(g, carry):
            span = pl.ds(pl.multiple_of(g * GROUP, GROUP), GROUP)
            z = part[m, col, span, :]
            for step in range(1, col_count):
                z += landed[m, around(col, step, col_count), span, :]
            y = jax.nn.gelu(z, approximate=True)
            active[span, :] = y
            squares[span, :] = jnp.broadcast_to(jnp.sum(y * y, axis=1, keepdims=True), (GROUP, 128))
            return carry
        lax.fori_loop(0, rows // GROUP, activate, 0)

        def share(own, outgoing, incoming, send, recv, axis, position, count):
            outgoing[m] = own
            copies = []
            for step in range(1, count):
                target = around(position, step, count)
                copies.append(remote(outgoing.at[m], incoming.at[m, position], send.at[m, target],
                                     recv.at[m, position], {axis: target}))
                copies[-1].start()
            total = own
            for step in range(1, count):
                source = around(position, step, count)
                remote(outgoing.at[m], incoming.at[m, source], send.at[m, source],
                       recv.at[m, source], {axis: source}).wait_recv()
                total = total + incoming[m, source]
            for copy in copies:
                copy.wait_send()
            return total

        total = squares[...].T[:8]
        total = share(total, col_out, col_in, col_send, col_recv, "col", col, col_count)
        total = share(total, row_out, row_in, row_send, row_recv, "row", row, row_count)
        scale = lax.rsqrt(total[:1] / total_features + 1e-06)
        squares[...] = jnp.broadcast_to(scale, (128, rows)).T

        def normalize(g, carry):
            span = pl.ds(pl.multiple_of(g * GROUP, GROUP), GROUP)
            o = active[span, :] * squares[span, :1] * gain_ref[...]
            out_ref[m, span, :] = o
            handing[m, span, :] = gathered[m, row, span, :] + o
            return carry
        lax.fori_loop(0, rows // GROUP, normalize, 0)

        @pl.when(section < sections - 1)
        def _():
            hand(m).start()

    def step_body(m, carry):
        @pl.when(m < micro)
        def _():
            multiply(m)

        @pl.when(m > 0)
        def _():
            finish(m - 1)
        return carry
    lax.fori_loop(0, micro + 1, step_body, 0)

    def drain(m, carry):
        for step in range(1, chips):
            gather_send(m, x_ref.at[m], chip_row(step, core)).wait_send()
            if cores == 2:
                gather_forward(m, step).wait_send()
        if cores == 2:
            gather_send(m, x_ref.at[m], chip * cores + 1 - core).wait_send()
        for step in range(1, col_count):
            chunk_send(m, around(col, step, col_count)).wait_send()

        @pl.when(section < sections - 1)
        def _():
            hand(m).wait_send()
        return carry
    lax.fori_loop(0, micro, drain, 0)


def solution(mesh):
    sections, row_count, col_count = (mesh.shape[name] for name in ("section", "row", "col"))

    def shards(inputs, weights, norm_gain):
        micro, rows, pieces = inputs.shape
        depth = row_count * pieces
        out_cols = weights.shape[4]
        width = min(256, pieces)
        f32 = jnp.float32
        dma = pltpu.SemaphoreType.DMA
        result = pl.pallas_call(
            functools.partial(kernel, sections, row_count, col_count),
            out_shape=jax.ShapeDtypeStruct((micro, rows, pieces), f32),
            in_specs=[
                pl.BlockSpec(memory_space=pltpu.VMEM),
                pl.BlockSpec(memory_space=pltpu.HBM),
                pl.BlockSpec(memory_space=pltpu.VMEM),
            ],
            out_specs=pl.BlockSpec(memory_space=pltpu.VMEM),
            scratch_shapes=[
                pltpu.VMEM((micro, row_count, rows, pieces), f32),
                pltpu.VMEM((row_count, 2 * rows, pieces), jnp.bfloat16),
                pltpu.VMEM((micro, col_count, rows, pieces), f32),
                pltpu.VMEM((micro, col_count, rows, pieces), f32),
                pltpu.VMEM((rows, pieces), f32),
                pltpu.VMEM((rows, 128), f32),
                pltpu.VMEM((micro, rows, pieces), f32),
                pltpu.VMEM((micro, rows, pieces), f32),
                pltpu.VMEM((SLOTS, depth, width), f32),
                pltpu.VMEM((micro, 8, rows), f32),
                pltpu.VMEM((micro, col_count, 8, rows), f32),
                pltpu.VMEM((micro, 8, rows), f32),
                pltpu.VMEM((micro, row_count, 8, rows), f32),
                dma((SLOTS,)),
                dma((micro, row_count)),
                dma((micro, row_count)),
                dma((micro, col_count)),
                dma((micro, col_count)),
                dma((micro, col_count)),
                dma((micro, col_count)),
                dma((micro, row_count)),
                dma((micro, row_count)),
                dma((micro,)),
                dma((micro,)),
            ],
            compiler_params=pltpu.CompilerParams(
                collective_id=0, has_side_effects=True, vmem_limit_bytes=60 * 1024 * 1024
            ),
        )(inputs, weights.reshape(depth, out_cols), norm_gain)
        return result[None]

    placed = (
        P(None, None, ("row", "col")),
        P("section", None, "col", None, "row"),
        P("section", ("row", "col")),
    )
    return jax.shard_map(
        shards,
        mesh=mesh,
        in_specs=placed,
        out_specs=P("section", None, None, ("row", "col")),
        check_vma=False,
    )
```

time: 660 us -> 342 us (0.52)
  Pallas kernels: 0 us -> 339 us
  waiting for transfers between devices: 281 us -> 0 us
  matrix products: 133 us -> 0 us
  blocking collectives: 116 us -> 0 us
  other arithmetic: 99.5 us -> 0 us
  between operations: 13.7 us -> 0.01 us
    pallas_call x0 -> x1, Pallas kernels: none -> 339 us  [shards(): pl.pallas_call(functools.partial(kernel, sections, row_count, col_count),...]
    reduce_scatter x4 -> x0, waiting for transfers between devices: 170 us -> none  [shards(): lax.psum_scatter(partial_value, 'col', scatter_dimension=1, tiled=True)]
    dot_general x8 -> x0, matrix products: 133 us -> none  [the longest x4 70 us: shards(): prod_two = jnp.dot(first, wsecond, preferred_element_type=jnp.float32)]
    psum x4 -> x0, blocking collectives: 116 us -> none  [shards(): squares = lax.psum(jnp.sum(active * active, axis=1), ('row', 'col'))]
    convert_element_type x10 -> x0, other arithmetic: 83.6 us -> none  [the longest x5 43.2 us: split_two(): (values - first.astype(jnp.float32)).astype(jnp.bfloat16)]
    all_gather x4 -> x0, waiting for transfers between devices: 78.3 us -> none  [shards(): lax.all_gather(current, 'row', axis=1, tiled=True)]
    ppermute x3 -> x0, waiting for transfers between devices: 32 us -> none  [from_behind(): lax.ppermute(value, axis, [(source, source + steps) for source in range(i...]
    dynamic_update_slice x4 -> x0, other arithmetic: 6.96 us -> none  [shards(): lax.dynamic_update_index_in_dim(results, jnp.where(valid, normed, former)...]
  transfers between devices with their start and end apart: 11 -> 0, of which waited for: 10 -> 0; matrix products, arithmetic and copies ran while one was open for 12% -> 0% of each run, Pallas kernels for 0% -> 0%
where the time goes in v1:
time: 342 us
  Pallas kernels  339 us (99%)
    pallas_call x1, Pallas kernels, shards(): pl.pallas_call(functools.partial(kernel, sections, row_count, col_count),...  339 us

profile of v1, /device:TPU:5, one launch (start us, length us, event | category | flops | bytes accessed | tf_op | source)
XLA Modules:
  0.0 341.7 jit_solution(16028113854324109294)
XLA Ops:
  0.0 339.0 %shard_map.37 = f32[3,128,1024]{2,1,0:T(8,128)} custom-call(f32[3,128,1024]{2,1,0:T(8,128)} %x_ref.1, f32[4096,4096]{1,0:T(8,128)} %bitcast.w_ref, f32[1,1024]{1,0:T(1,128)} %gain_ref.1), custom_call_target="tpu_custom_call" | custom-call | tf_op jit(solution)/shard_map/pallas_call | solution.py:261
  339.0 2.7 copy.5
